TPU v7x, 32 devices: a whole 2x2x4 slice. The times are simulated.
32 devices in a mesh: batch: 8 (over z, y), mp: 4 (over x, core).
Axes of the slice: x: 2, y: 2, z: 4, core: 2. Of those that a mesh axis runs over, the one named last changes fastest.
Arguments:
- init_state: float32 [4096, 256], P(('batch', 'mp')), may hold values from -6 to 6
- brownian: bfloat16 [32, 4096, 256], P(None, ('batch', 'mp')), may hold values from -6 to 6
- step_size: float32 [4096], P(('batch', 'mp')), may hold values from 0.02 to 0.1
- lengths: int32 [4096], P(('batch', 'mp')), may hold values from 1 to 32, as said below
- obs_steps: int32 [4096, 8], P(('batch', 'mp')), may hold values from 1 to 32, as said below
- observed: bfloat16 [4096, 8, 128], P(('batch', 'mp')), may hold values from -6 to 6
- w_in: bfloat16 [256, 1024], P(None, 'mp'), may hold values from -0.375 to 0.375
- b_in: bfloat16 [1024], P('mp'), may hold values from -3 to 3
- w_out: bfloat16 [1024, 256], P('mp'), may hold values from -0.1875 to 0.1875
- b_out: float32 [256], replicated, may hold values from -4 to 4
- decoder: bfloat16 [256, 128], replicated, may hold values from -0.375 to 0.375
- prior_rate: float32 [256], replicated, may hold values from 0.1 to 2
- diffusion: float32 [256], replicated, may hold values from 0.7 to 1.4
Outputs:
- elbo_series: float32 [4096], P(('batch', 'mp'))
- scores: float32 [2], replicated
- grad_w_in: float32 [256, 1024], P(None, 'mp')
- grad_b_in: float32 [1024], P('mp')
- grad_w_out: float32 [1024, 256], P('mp')
- grad_b_out: float32 [256], replicated
- grad_decoder: float32 [256, 128], replicated
- grad_init: float32 [4096, 256], P(('batch', 'mp'))
Inputs may be any that keep to these rules, and one draw needn't show every extreme that they name: `lengths`: some series has 32 live steps in every draw. obs_steps[i, j] is at most lengths[i].
All inputs are finite; a program needn't handle non-finite values.
Results may differ from a plain program's by a relative error of at most 0.0019.
Values may be sent and summed in bfloat16 or wider, within the bound.
A program may use at most 64 MiB of HBM per device.

v0:
```python
import jax
import jax.numpy as jnp
from jax import lax
from jax.experimental import pallas as pl
from jax.experimental.pallas import tpu as pltpu
from jax.sharding import PartitionSpec as P

F32 = jnp.float32
BF16 = jnp.bfloat16
NT = (((1,), (1,)), ((), ()))


def dot(a, b):
    return jnp.dot(a, b, preferred_element_type=F32)


def dot_nt(a, b):
    return lax.dot_general(a, b, NT, preferred_element_type=F32)


def fold(value):
    return value.reshape(-1, 8, value.shape[1]).sum(axis=0)


def core_kernel(
    init_ref,
    noise_ref,
    step_ref,
    length_ref,
    obs_ref,
    seen_ref,
    w_in_ref,
    b_in_ref,
    w_out_ref,
    b_out_ref,
    dec_ref,
    rate_ref,
    diff_ref,
    elbo_ref,
    grads_ref,
    cot_ref,
    x_ref,
    xt_ref,
    ut_ref,
    act_ref,
    pre_ref,
    scaled_ref,
    pick_ref,
    obs_wide_ref,
    dt_ref,
    root_ref,
    len_ref,
    state_ref,
    kl_ref,
    sum_b_in_ref,
    sum_b_out_ref,
    miss_ref,
    target_ref,
):
    rows, width = init_ref.shape
    steps = noise_ref.shape[0]
    seen_count = obs_ref.shape[0]
    seen_width = dec_ref.shape[1]
    chunks = w_in_ref.shape[0]

    def column(row):
        return jnp.broadcast_to(row, (rows, rows)).T

    dt_ref[...] = column(step_ref[...])
    root_ref[...] = jnp.sqrt(dt_ref[...])
    len_ref[...] = column(length_ref[...])
    for j in range(seen_count):
        obs_wide_ref[j] = column(obs_ref[j : j + 1, :])
    target_ref[...] = seen_ref[...].astype(F32).reshape(target_ref.shape)
    pick_ref[...] = jnp.zeros_like(pick_ref)
    kl_ref[...] = jnp.zeros_like(kl_ref)
    sum_b_in_ref[...] = jnp.zeros_like(sum_b_in_ref)
    sum_b_out_ref[...] = jnp.zeros_like(sum_b_out_ref)
    state_ref[...] = init_ref[...]
    x_ref[0] = init_ref[...].astype(BF16)

    def both(value):
        return jnp.concatenate([value] * (width // rows), axis=1)

    def forward(k, carry):
        x = x_ref[k]
        drift = jnp.broadcast_to(b_out_ref[...], (rows, width))
        for n in range(chunks):
            act = jnp.tanh(dot(x, w_in_ref[n]) + b_in_ref[n, :1, :]).astype(BF16)
            act_ref[n, pl.ds(k * rows, rows), :] = act
            drift = drift + dot(act, w_out_ref[n])
        state = state_ref[...]
        inv = 1.0 / diff_ref[...]
        live = k < len_ref[...]
        factor = both(jnp.where(live, dt_ref[...], 0.0))
        root = both(jnp.where(live, root_ref[...], 0.0))
        residual = (drift + rate_ref[...] * state) * inv
        kl_ref[...] += factor * residual * residual
        scaled_ref[k] = residual * inv
        following = state + (
            factor * drift + diff_ref[...] * root * noise_ref[k].astype(F32)
        )
        state_ref[...] = following
        rounded = following.astype(BF16)
        x_ref[k + 1] = rounded
        xt_ref[:, pl.ds(pl.multiple_of(k * rows, rows), rows)] = x.T
        seen = dot(rounded, dec_ref[...])
        for j in range(seen_count):
            pick_ref[j] = jnp.where(obs_wide_ref[j] == k + 1, seen, pick_ref[j])
        return carry

    lax.fori_loop(0, steps, forward, 0)

    square = jnp.zeros((rows, seen_width), F32)
    for j in range(seen_count):
        misfit = pick_ref[j] - target_ref[pl.ds(j, rows, stride=seen_count), :]
        square = square + misfit * misfit
        pick_ref[j] = misfit.astype(BF16).astype(F32)
    loglik = -0.5 * jnp.sum(square.T, axis=0, keepdims=True)
    kl_half = kl_ref[:, :rows]
    for part in range(1, width // rows):
        kl_half = kl_half + kl_ref[:, part * rows : (part + 1) * rows]
    kl_row = 0.5 * jnp.sum(kl_half.T, axis=0, keepdims=True)
    divisor = (width * length_ref[...] + seen_width * seen_count).astype(F32)
    elbo_ref[...] = (loglik - kl_row) / divisor

    cot_ref[...] = jnp.zeros_like(cot_ref)

    def backward(index, carry):
        k = steps - 1 - index
        total = jnp.zeros((rows, seen_width), F32)
        for j in range(seen_count):
            total = total + jnp.where(obs_wide_ref[j] == k + 1, pick_ref[j], 0.0)
        high = total.astype(BF16)
        low = (total - high.astype(F32)).astype(BF16)
        miss_ref[pl.ds(k * rows, rows), :seen_width] = high
        miss_ref[pl.ds(k * rows, rows), seen_width:] = low
        obs_back = dot_nt(high, dec_ref[...]) + dot_nt(low, dec_ref[...])
        cot = cot_ref[...] + obs_back
        scaled = scaled_ref[k]
        factor = both(jnp.where(k < len_ref[...], dt_ref[...], 0.0))
        update = factor * (cot + scaled)
        rounded = update.astype(BF16)
        ut_ref[:, pl.ds(pl.multiple_of(k * rows, rows), rows)] = rounded.T
        sum_b_out_ref[...] += fold(update)
        cot = cot + factor * rate_ref[...] * scaled
        for n in range(chunks):
            act = act_ref[n, pl.ds(k * rows, rows), :].astype(F32)
            pre = dot_nt(rounded, w_out_ref[n]) * (1.0 - act * act)
            sum_b_in_ref[n] += fold(pre)
            pre_round = pre.astype(BF16)
            pre_ref[n, pl.ds(k * rows, rows), :] = pre_round
            cot = cot + dot_nt(pre_round, w_in_ref[n])
        cot_ref[...] = cot
        return carry

    lax.fori_loop(0, steps, backward, 0)

    def gradients(n, carry):
        grads_ref[n, :width, :] = dot(xt_ref[...], pre_ref[n])
        grads_ref[n, width : 2 * width, :] = dot(ut_ref[...], act_ref[n]).T
        return carry

    lax.fori_loop(0, chunks, gradients, 0)

    dec_grad = jnp.zeros((width, 2 * seen_width), F32)
    dec_grad = dec_grad + dot(xt_ref[:, rows:], miss_ref[: (steps - 1) * rows, :])
    last = lax.dot_general(
        x_ref[steps],
        miss_ref[(steps - 1) * rows :, :],
        (((0,), (0,)), ((), ())),
        preferred_element_type=F32,
    )
    dec_grad = dec_grad + last
    dec_grad = dec_grad[:, :seen_width] + dec_grad[:, seen_width:]
    lanes = width // seen_width
    share = width // chunks
    tail = 2 * width
    line = tail + share // lanes
    for n in range(chunks):
        pieces = [
            dec_grad[n * share + m * share // lanes : n * share + (m + 1) * share // lanes, :]
            for m in range(lanes)
        ]
        grads_ref[n, tail:line, :] = jnp.concatenate(pieces, axis=1)
        grads_ref[n, line:, :] = jnp.zeros((grads_ref.shape[1] - line, width), F32)
        grads_ref[n, line : line + 1, :] = jnp.sum(sum_b_in_ref[n], axis=0, keepdims=True)
        grads_ref[n, line + 1 : line + 2, :] = jnp.sum(
            sum_b_out_ref[...], axis=0, keepdims=True
        )
        grads_ref[n, line + 2 : line + 3, :rows] = loglik
        grads_ref[n, line + 2 : line + 3, rows : 2 * rows] = kl_row


def core(grad_rows, init, noise, step, length, obs, seen, w_in, b_in, w_out, b_out, dec, rate, diff):
    rows, width = init.shape
    steps = noise.shape[0]
    seen_count, seen_width = seen.shape[1], dec.shape[1]
    chunks = w_in.shape[0]
    vmem = pl.BlockSpec(memory_space=pltpu.VMEM)
    out = [
        jax.ShapeDtypeStruct((1, rows), F32),
        jax.ShapeDtypeStruct((chunks, grad_rows, width), F32),
        jax.ShapeDtypeStruct((rows, width), F32),
    ]
    resident = (6, 7, 8)
    operands = (init, noise, step, length, obs, seen, w_in, b_in, w_out, b_out, dec, rate, diff)
    loaded = [i for i in range(len(operands)) if i not in resident]
    specs = [
        vmem if i in resident else pl.BlockSpec(memory_space=pltpu.HBM)
        for i in range(len(operands))
    ]

    def body(*refs):
        refs = list(refs)
        sems = refs.pop()
        spaces = [refs.pop() for _ in loaded][::-1]
        copies = []
        for at, (i, space) in enumerate(zip(loaded, spaces)):
            copy = pltpu.make_async_copy(refs[i], space, sems.at[at])
            copy.start()
            copies.append(copy)
            refs[i] = space
        for copy in copies:
            copy.wait()
        core_kernel(*refs)

    scratch = [
        pltpu.VMEM((steps + 1, rows, width), BF16),
        pltpu.VMEM((width, steps * rows), BF16),
        pltpu.VMEM((width, steps * rows), BF16),
        pltpu.VMEM((chunks, steps * rows, width), BF16),
        pltpu.VMEM((chunks, steps * rows, width), BF16),
        pltpu.VMEM((steps, rows, width), F32),
        pltpu.VMEM((seen_count, rows, seen_width), F32),
        pltpu.VMEM((seen_count, rows, rows), jnp.int32),
        pltpu.VMEM((rows, rows), F32),
        pltpu.VMEM((rows, rows), F32),
        pltpu.VMEM((rows, rows), jnp.int32),
        pltpu.VMEM((rows, width), F32),
        pltpu.VMEM((rows, width), F32),
        pltpu.VMEM((chunks, 8, width), F32),
        pltpu.VMEM((8, width), F32),
        pltpu.VMEM((steps * rows, 2 * seen_width), BF16),
        pltpu.VMEM((rows * seen_count, seen_width), F32),
    ]
    scratch += [pltpu.VMEM(operands[i].shape, operands[i].dtype) for i in loaded]
    scratch += [pltpu.SemaphoreType.DMA((len(loaded),))]
    return pl.pallas_call(
        body,
        out_shape=out,
        in_specs=specs,
        out_specs=[vmem] * 3,
        scratch_shapes=scratch,
        compiler_params=pltpu.CompilerParams(vmem_limit_bytes=60 * 1024 * 1024),
        cost_estimate=pl.CostEstimate(
            flops=12 * steps * rows * width * width * chunks,
            bytes_accessed=8 << 20,
            transcendentals=steps * rows * width * chunks,
        ),
        name="sde",
    )(*operands)


def send(source, target, send_sem, recv_sem, peer):
    return pltpu.make_async_remote_copy(
        src_ref=source,
        dst_ref=target,
        send_sem=send_sem,
        recv_sem=recv_sem,
        device_id=peer,
        device_id_type=pl.DeviceIdType.MESH,
    )


def greet(peers):
    barrier = pltpu.get_barrier_semaphore()
    for peer in peers:
        pl.semaphore_signal(barrier, inc=1, device_id=peer, device_id_type=pl.DeviceIdType.MESH)
    pl.semaphore_wait(barrier, len(peers))


def mp_places():
    mine = lax.axis_index("mp")
    chip, unit = mine // 2, mine % 2
    sibling = chip * 2 + (1 - unit)
    across = (1 - chip) * 2 + unit
    diagonal = (1 - chip) * 2 + (1 - unit)
    return mine, sibling, across, diagonal


def gather_kernel(w_in_ref, w_out_ref, b_in_ref, all_in_ref, all_out_ref, all_b_ref, bias_ref, send_sem, recv_sem):
    mine, sibling, across, diagonal = mp_places()
    batch = lax.axis_index("batch")
    to_across, to_sibling = (batch, across), (batch, sibling)
    bias_ref[...] = jnp.broadcast_to(b_in_ref[...].astype(F32), bias_ref.shape)
    greet([to_across, to_sibling])
    pairs = ((w_in_ref, all_in_ref), (w_out_ref, all_out_ref), (bias_ref, all_b_ref))
    far, near, relayed = [], [], []
    for i, (own, whole) in enumerate(pairs):
        copy = send(own, whole.at[mine], send_sem.at[0, i], recv_sem.at[0, i], to_across)
        copy.start()
        far.append(copy)
    for i, (own, whole) in enumerate(pairs):
        copy = send(own, whole.at[mine], send_sem.at[1, i], recv_sem.at[1, i], to_sibling)
        copy.start()
        near.append(copy)
    for own, whole in pairs:
        whole[mine] = own[...]
    for i, (own, whole) in enumerate(pairs):
        far[i].wait_recv()
        copy = send(
            whole.at[across], whole.at[across], send_sem.at[2, i], recv_sem.at[2, i], to_sibling
        )
        copy.start()
        relayed.append(copy)
    for copy in far:
        copy.wait_send()
    for copy in near + relayed:
        copy.wait()


def gather(w_in, w_out, b_in):
    count = lax.axis_size("mp")
    vmem = pl.BlockSpec(memory_space=pltpu.VMEM)
    return pl.pallas_call(
        gather_kernel,
        out_shape=[
            jax.ShapeDtypeStruct((count,) + w_in.shape, BF16),
            jax.ShapeDtypeStruct((count,) + w_out.shape, BF16),
            jax.ShapeDtypeStruct((count, 8, b_in.shape[1]), F32),
        ],
        in_specs=[vmem] * 3,
        out_specs=[vmem] * 3,
        scratch_shapes=[
            pltpu.VMEM((8, b_in.shape[1]), F32),
            pltpu.SemaphoreType.DMA((3, 3)),
            pltpu.SemaphoreType.DMA((3, 3)),
        ],
        compiler_params=pltpu.CompilerParams(
            collective_id=0, has_side_effects=True, vmem_limit_bytes=8 * 1024 * 1024
        ),
        cost_estimate=pl.CostEstimate(flops=0, bytes_accessed=32 << 20, transcendentals=0),
        name="gather_weights",
    )(w_in, w_out, b_in)


def reduce_kernel(
    members,
    total,
    grads_ref,
    done_ref,
    decs_ref,
    near_ref,
    far_w_ref,
    far_t_ref,
    got_w_ref,
    got_t_ref,
    full_ref,
    round_ref,
    parts_ref,
    near_send,
    near_recv,
    far_send,
    far_recv,
    rs_send,
    rs_recv,
    ag_send,
    ag_recv,
    pair_send,
    pair_recv,
    dec_send,
    dec_recv,
):
    mine, sibling, across, diagonal = mp_places()
    batch = lax.axis_index("batch")
    width = grads_ref.shape[2]
    weight_rows = 2 * width
    piece = grads_ref.shape[1] // members
    others = [(lax.rem(batch + d, members), mine) for d in range(1, members)]
    group = [(batch, sibling), (batch, across), (batch, diagonal)]
    greet(group + others)
    near = []
    for i, quarter in enumerate((diagonal, sibling)):
        copy = send(
            grads_ref.at[quarter], near_ref.at[i], near_send.at[i], near_recv.at[i], group[0]
        )
        copy.start()
        near.append(copy)
    near[0].wait_recv()
    far_w_ref[...] = (
        grads_ref[across, :weight_rows, :] + near_ref[0, :weight_rows, :]
    ).astype(BF16)
    far_t_ref[...] = grads_ref[across, weight_rows:, :] + near_ref[0, weight_rows:, :]
    far = [
        send(far_w_ref, got_w_ref, far_send.at[0], far_recv.at[0], group[1]),
        send(far_t_ref, got_t_ref, far_send.at[1], far_recv.at[1], group[1]),
    ]
    for copy in far:
        copy.start()
    near[1].wait_recv()
    full_ref[...] = grads_ref[mine] + near_ref[1]
    far[0].wait_recv()
    full_ref[:weight_rows, :] += got_w_ref[...].astype(F32)
    far[1].wait_recv()
    full_ref[weight_rows:, :] += got_t_ref[...]
    for p in range(members):
        round_ref[p] = full_ref[p * piece : (p + 1) * piece, :].astype(BF16)
    scatter = []
    for d in range(1, members):
        target = lax.rem(batch + d, members)
        copy = send(
            round_ref.at[target],
            parts_ref.at[d - 1],
            rs_send.at[d - 1],
            rs_recv.at[d - 1],
            others[d - 1],
        )
        copy.start()
        scatter.append(copy)
    here = pl.ds(pl.multiple_of(batch * piece, 8), piece)
    value = full_ref[here, :]
    for d in range(1, members):
        scatter[d - 1].wait_recv()
        value = value + parts_ref[d - 1].astype(F32)
    done_ref[here, :] = value / total
    pair = batch + 1 - 2 * (batch % 2)
    partner = (pair, mine)

    def rows_of(owner):
        return done_ref.at[pl.ds(pl.multiple_of(owner * piece, 8), piece), :]

    def relay(i, owner):
        return send(rows_of(owner), rows_of(owner), pair_send.at[i], pair_recv.at[i], partner)

    hops = members // 2
    spread = []
    for d in range(1, hops):
        target = lax.rem(batch + 2 * d, members)
        copy = send(
            rows_of(batch), rows_of(batch), ag_send.at[d - 1], ag_recv.at[d - 1], (target, mine)
        )
        copy.start()
        spread.append(copy)
    passed = [relay(0, batch)]
    passed[0].start()
    for copy in near + far + scatter:
        copy.wait_send()
    for d in range(1, hops):
        origin = lax.rem(batch + members - 2 * d, members)
        send(
            rows_of(origin),
            rows_of(origin),
            ag_send.at[d - 1],
            ag_recv.at[d - 1],
            (origin, mine),
        ).wait_recv()
        copy = relay(d, origin)
        copy.start()
        passed.append(copy)
    for d in range(hops):
        relay(d, lax.rem(pair + members - 2 * d, members)).wait_recv()
    spread += passed
    dec_rows = decs_ref.shape[1]
    exchange = []
    for i in range(3):
        copy = send(
            done_ref.at[pl.ds(weight_rows, dec_rows), :],
            decs_ref.at[mine],
            dec_send.at[i],
            dec_recv.at[i],
            group[i],
        )
        copy.start()
        exchange.append(copy)
    decs_ref[mine] = done_ref[weight_rows : weight_rows + dec_rows, :]
    for copy in spread:
        copy.wait_send()
    for i, origin in enumerate((sibling, across, diagonal)):
        exchange[i].wait_send()
        send(
            decs_ref.at[origin], decs_ref.at[origin], dec_send.at[i], dec_recv.at[i], group[i]
        ).wait_recv()


def finish_kernel(
    half, done_ref, decs_ref, w_in_ref, w_out_ref, b_in_ref, b_out_ref, dec_ref, scores_ref
):
    width = done_ref.shape[1]
    weight_rows = 2 * width
    dec_rows = decs_ref.shape[1]
    line = weight_rows + dec_rows
    w_in_ref[...] = done_ref[:width, :]
    w_out_ref[...] = done_ref[width:weight_rows, :]
    b_in_ref[...] = done_ref[line : line + 1, :]
    b_out_ref[...] = done_ref[line + 1 : line + 2, :]
    scores_ref[:, 0:1] = jnp.sum(done_ref[line + 2 : line + 3, :half], axis=1, keepdims=True)
    scores_ref[:, 1:2] = jnp.sum(
        done_ref[line + 2 : line + 3, half : 2 * half], axis=1, keepdims=True
    )
    seen_width = dec_ref.shape[1]
    for n in range(decs_ref.shape[0]):
        for m in range(width // seen_width):
            start = (n * (width // seen_width) + m) * dec_rows
            dec_ref[start : start + dec_rows, :] = decs_ref[
                n, :, m * seen_width : (m + 1) * seen_width
            ]


def reduce_all(grads, rows, seen_width):
    quarters, grad_rows, width = grads.shape
    members = lax.axis_size("batch")
    total = rows * members * lax.axis_size("mp")
    dec_rows = width // quarters // (width // seen_width)
    tail_rows = grad_rows - 2 * width
    piece = grad_rows // members
    vmem = pl.BlockSpec(memory_space=pltpu.VMEM)
    sems = []
    for count in (2, 2, members - 1, members // 2, members // 2, 3):
        sems += [pltpu.SemaphoreType.DMA((count,))] * 2

    def body(*refs):
        reduce_kernel(members, total, *refs)

    done, decs = pl.pallas_call(
        body,
        out_shape=[
            jax.ShapeDtypeStruct((grad_rows, width), F32),
            jax.ShapeDtypeStruct((quarters, dec_rows, width), F32),
        ],
        in_specs=[vmem],
        out_specs=[vmem] * 2,
        scratch_shapes=[
            pltpu.VMEM((2, grad_rows, width), F32),
            pltpu.VMEM((2 * width, width), BF16),
            pltpu.VMEM((tail_rows, width), F32),
            pltpu.VMEM((2 * width, width), BF16),
            pltpu.VMEM((tail_rows, width), F32),
            pltpu.VMEM((grad_rows, width), F32),
            pltpu.VMEM((members, piece, width), BF16),
            pltpu.VMEM((members - 1, piece, width), BF16),
        ]
        + sems,
        compiler_params=pltpu.CompilerParams(
            collective_id=1, has_side_effects=True, vmem_limit_bytes=16 * 1024 * 1024
        ),
        name="reduce_grads",
    )(grads)

    def finish(*refs):
        finish_kernel(rows, *refs)

    return pl.pallas_call(
        finish,
        out_shape=[
            jax.ShapeDtypeStruct((width, width), F32),
            jax.ShapeDtypeStruct((width, width), F32),
            jax.ShapeDtypeStruct((1, width), F32),
            jax.ShapeDtypeStruct((1, width), F32),
            jax.ShapeDtypeStruct((width, seen_width), F32),
            jax.ShapeDtypeStruct((1, 2), F32),
        ],
        in_specs=[vmem] * 2,
        out_specs=[vmem] * 6,
        compiler_params=pltpu.CompilerParams(vmem_limit_bytes=8 * 1024 * 1024),
        name="finish",
    )(done, decs)


def on_device(
    init_state,
    brownian,
    step_size,
    lengths,
    obs_steps,
    observed,
    w_in,
    b_in,
    w_out,
    b_out,
    decoder,
    prior_rate,
    diffusion,
):
    rows, width = init_state.shape
    seen_width = decoder.shape[1]
    w_in_all, w_out_all, b_in_all = gather(w_in, w_out, b_in[None, :])
    unit = 8 * lax.axis_size("batch")
    need = 2 * width + width // lax.axis_size("mp") * seen_width // width + 3
    elbo, grads, cot = core(
        -(-need // unit) * unit,
        init_state,
        brownian,
        step_size[None, :],
        lengths[None, :],
        obs_steps.T,
        observed,
        w_in_all,
        b_in_all,
        w_out_all,
        b_out[None, :],
        decoder,
        prior_rate[None, :],
        diffusion[None, :],
    )
    own_w_in, own_w_out, own_b_in, b_out_grad, dec_grad, scores = reduce_all(
        grads, rows, seen_width
    )
    return (
        elbo[0],
        scores[0],
        own_w_in,
        own_b_in[0],
        own_w_out,
        b_out_grad[0],
        dec_grad,
        cot,
    )


def solution(mesh):
    both = ("batch", "mp")
    placed = (
        P(both, None),
        P(None, both, None),
        P(both),
        P(both),
        P(both, None),
        P(both, None, None),
        P(None, "mp"),
        P("mp"),
        P("mp", None),
        P(),
        P(),
        P(),
        P(),
    )
    return jax.shard_map(
        on_device,
        mesh=mesh,
        in_specs=placed,
        out_specs=(
            P(both),
            P(),
            P(None, "mp"),
            P("mp"),
            P("mp", None),
            P(),
            P(),
            P(both, None),
        ),
        check_vma=False,
    )
```

profile of v0, /device:TPU:0, one launch (start us, length us, event | category | flops | bytes accessed | tf_op | source)
XLA Modules:
  0.0 105.9 jit_solution(6791156246216542246)
XLA Ops:
  0.6 0.7 broadcast_in_dim.20.b_in_ref
  1.3 0.0 copy-start.1
  1.3 0.9 copy-done.1
  2.2 0.0 copy-start.2
  2.2 0.9 copy-done.2
  3.1 11.2 %gather_weights.1 = (bf16[4,256,256]{2,1,0:T(8,128)(2,1)S(1)}, bf16[4,256,256]{2,1,0:T(8,128)(2,1)S(1)}, f32[4,8,256]{2,1,0:T(8,128)S(1)}) custom-call(bf16[256,256]{1,0:T(8,128)(2,1)S(1)} %copy-done.1, bf16[256,256]{1,0:T(8,128)(2,1)S(1)} %copy-done.2, bf16[1,256]{1,0:T(2,128)(2,1)S(1)} %broadcast_in_dim.20.b_in_ref), custom_call_target="tpu_custom_call" | custom-call | bytes 33554432 | tf_op jit(solution)/shard_map/gather_weights/pallas_call | solution.py:326
  14.3 0.0 copy-start.3
  14.3 0.8 copy-done.3
  15.1 0.0 copy-start.4
  15.1 0.8 copy-done.4
  15.9 0.0 copy-start.5
  15.9 0.6 copy-done.5
  16.5 49.6 %sde.1 = (f32[1,128]{1,0:T(1,128)}, f32[4,576,256]{2,1,0:T(8,128)}, f32[128,256]{1,0:T(8,128)}) custom-call(f32[128,256]{1,0:T(8,128)} %refs_0_.1, bf16[32,128,256]{2,1,0:T(8,128)(2,1)} %refs_1_.1, f32[1,128]{1,0:T(1,128)} %bitcast.16, s32[1,128]{1,0:T(1,128)} %bitcast.17, s32[8,128]{1,0:T(8,128)} %bitcast.10, bf16[128,8,128]{2,1,0:T(8,128)(2,1)} %refs_5_.1, ...), custom_call_target="tpu_custom_call" | custom-call | flops 12884901888 | bytes 8388608 | tf_op jit(solution)/shard_map/sde/pallas_call | solution.py:249
  66.1 0.0 copy-start
  66.2 1.7 %copy-done = f32[4,576,256]{2,1,0:T(8,128)S(1)} copy-done((f32[4,576,256]{2,1,0:T(8,128)S(1)}, f32[4,576,256]{2,1,0:T(8,128)}, u32[]{:S(2)}) %copy-start) | copy-done | bytes 2359320
  67.8 37.2 %reduce_grads.1 = (f32[576,256]{1,0:T(8,128)S(1)}, f32[4,32,256]{2,1,0:T(8,128)S(1)}) custom-call(f32[4,576,256]{2,1,0:T(8,128)S(1)} %copy-done), custom_call_target="tpu_custom_call" | custom-call | tf_op jit(solution)/shard_map/reduce_grads/pallas_call | solution.py:525
  105.1 0.9 finish.1
Async XLA Ops:
  1.3 0.9 copy-start.1
  2.2 0.9 copy-start.2
  14.3 0.8 copy-start.3
  15.1 0.8 copy-start.4
  15.9 0.6 copy-start.5
  66.1 1.7 %copy-start = (f32[4,576,256]{2,1,0:T(8,128)S(1)}, f32[4,576,256]{2,1,0:T(8,128)}, u32[]{:S(2)}) copy-start(f32[4,576,256]{2,1,0:T(8,128)} %get-tuple-element.26.refs_0_) | copy-start | bytes 7077892
where the time goes:
time: 106 us
  Pallas kernels  98.9 us (93%)
  local copies, waits for them, and re-layouts  6.32 us (6%)
    pallas_call x1, Pallas kernels, core(): pl.pallas_call(body, out_shape=out, in_specs=specs, out_specs=[vmem] * 3,...  49.6 us
    pallas_call x1, Pallas kernels, reduce_all(): pl.pallas_call(body, out_shape=[jax.ShapeDtypeStruct((grad_rows, width),...  37.2 us
    pallas_call x1, Pallas kernels, gather(): pl.pallas_call(gather_kernel, out_shape=[jax.ShapeDtypeStruct((count,) +...  11.2 us
    unnamed x12, local copies, waits for them, and re-layouts  5.66 us

commit v1 on v0

--- a/solution.py
+++ b/solution.py
@@ -8,6 +8,8 @@
 F32 = jnp.float32
 BF16 = jnp.bfloat16
 NT = (((1,), (1,)), ((), ()))
+UNROLL_F = 2
+UNROLL_B = 2
 
 
 def dot(a, b):
@@ -56,6 +58,11 @@
     sum_b_out_ref,
     miss_ref,
     target_ref,
+    w_in_t_ref,
+    w_out_t_ref,
+    dec_t_ref,
+    w_in_wide_ref,
+    bias_ref,
 ):
     rows, width = init_ref.shape
     steps = noise_ref.shape[0]
@@ -66,6 +73,9 @@
     def column(row):
         return jnp.broadcast_to(row, (rows, rows)).T
 
+    for n in range(chunks):
+        w_in_wide_ref[:, n * width : (n + 1) * width] = w_in_ref[n]
+        bias_ref[:, n * width : (n + 1) * width] = b_in_ref[n, :1, :]
     dt_ref[...] = column(step_ref[...])
     root_ref[...] = jnp.sqrt(dt_ref[...])
     len_ref[...] = column(length_ref[...])
@@ -82,34 +92,47 @@
     def both(value):
         return jnp.concatenate([value] * (width // rows), axis=1)
 
+    def pick(index, seen):
+        for j in range(seen_count):
+            pick_ref[j] = jnp.where(obs_wide_ref[j] == index, seen, pick_ref[j])
+
+    def paired(values):
+        while len(values) > 2:
+            values = [values[i] + values[i + 2] for i in (0, 1)] + values[4:]
+        return values[0] + values[1]
+
     def forward(k, carry):
         x = x_ref[k]
-        drift = jnp.broadcast_to(b_out_ref[...], (rows, width))
-        for n in range(chunks):
-            act = jnp.tanh(dot(x, w_in_ref[n]) + b_in_ref[n, :1, :]).astype(BF16)
-            act_ref[n, pl.ds(k * rows, rows), :] = act
-            drift = drift + dot(act, w_out_ref[n])
+        raw = dot(x, w_in_wide_ref[...])
+        seen = dot(x, dec_ref[...])
+        act = jnp.tanh(raw + bias_ref[...]).astype(BF16)
+        act_ref[pl.ds(k * rows, rows), :] = act
+        drift = dot(act, w_out_ref[...].reshape(chunks * width, width)) + b_out_ref[...]
         state = state_ref[...]
         inv = 1.0 / diff_ref[...]
         live = k < len_ref[...]
         factor = both(jnp.where(live, dt_ref[...], 0.0))
         root = both(jnp.where(live, root_ref[...], 0.0))
-        residual = (drift + rate_ref[...] * state) * inv
-        kl_ref[...] += factor * residual * residual
-        scaled_ref[k] = residual * inv
         following = state + (
             factor * drift + diff_ref[...] * root * noise_ref[k].astype(F32)
         )
         state_ref[...] = following
-        rounded = following.astype(BF16)
-        x_ref[k + 1] = rounded
+        x_ref[k + 1] = following.astype(BF16)
+        residual = (drift + rate_ref[...] * state) * inv
+        kl_ref[...] += factor * residual * residual
+        scaled_ref[k] = residual * inv
         xt_ref[:, pl.ds(pl.multiple_of(k * rows, rows), rows)] = x.T
-        seen = dot(rounded, dec_ref[...])
-        for j in range(seen_count):
-            pick_ref[j] = jnp.where(obs_wide_ref[j] == k + 1, seen, pick_ref[j])
+        pick(k, seen)
         return carry
 
-    lax.fori_loop(0, steps, forward, 0)
+    lax.fori_loop(0, steps, forward, 0, unroll=UNROLL_F)
+    pick(steps, dot(x_ref[steps], dec_ref[...]))
+    for n in range(chunks):
+        w_in_t_ref[n * width : (n + 1) * width, :] = w_in_ref[n].T
+        w_out_t_ref[:, n * width : (n + 1) * width] = w_out_ref[n].T
+    dec_t = dec_ref[...].T
+    dec_t_ref[:seen_width, :] = dec_t
+    dec_t_ref[seen_width:, :] = dec_t
 
     square = jnp.zeros((rows, seen_width), F32)
     for j in range(seen_count):
@@ -124,50 +147,48 @@
     divisor = (width * length_ref[...] + seen_width * seen_count).astype(F32)
     elbo_ref[...] = (loglik - kl_row) / divisor
 
-    cot_ref[...] = jnp.zeros_like(cot_ref)
+    def obs_back(index):
+        total = jnp.zeros((rows, seen_width), F32)
+        for j in range(seen_count):
+            total = total + jnp.where(obs_wide_ref[j] == index, pick_ref[j], 0.0)
+        high = total.astype(BF16)
+        low = (total - high.astype(F32)).astype(BF16)
+        wide = jnp.concatenate([high, low], axis=1)
+        miss_ref[pl.ds(pl.multiple_of(index * rows, rows), rows), :] = wide
+        return dot(wide, dec_t_ref[...])
+
+    cot_ref[...] = obs_back(steps)
 
     def backward(index, carry):
         k = steps - 1 - index
-        total = jnp.zeros((rows, seen_width), F32)
-        for j in range(seen_count):
-            total = total + jnp.where(obs_wide_ref[j] == k + 1, pick_ref[j], 0.0)
-        high = total.astype(BF16)
-        low = (total - high.astype(F32)).astype(BF16)
-        miss_ref[pl.ds(k * rows, rows), :seen_width] = high
-        miss_ref[pl.ds(k * rows, rows), seen_width:] = low
-        obs_back = dot_nt(high, dec_ref[...]) + dot_nt(low, dec_ref[...])
-        cot = cot_ref[...] + obs_back
+        cot = cot_ref[...]
         scaled = scaled_ref[k]
         factor = both(jnp.where(k < len_ref[...], dt_ref[...], 0.0))
         update = factor * (cot + scaled)
         rounded = update.astype(BF16)
+        raw = dot(rounded, w_out_t_ref[...])
+        seen_back = obs_back(k)
+        act = act_ref[pl.ds(k * rows, rows), :].astype(F32)
+        pre = raw * (1.0 - act * act)
+        pre_round = pre.astype(BF16)
+        pre_ref[pl.ds(k * rows, rows), :] = pre_round
+        sum_b_in_ref[...] += fold(pre)
+        base = cot + factor * rate_ref[...] * scaled + seen_back
+        cot_ref[...] = dot(pre_round, w_in_t_ref[...]) + base
         ut_ref[:, pl.ds(pl.multiple_of(k * rows, rows), rows)] = rounded.T
         sum_b_out_ref[...] += fold(update)
-        cot = cot + factor * rate_ref[...] * scaled
-        for n in range(chunks):
-            act = act_ref[n, pl.ds(k * rows, rows), :].astype(F32)
-            pre = dot_nt(rounded, w_out_ref[n]) * (1.0 - act * act)
-            sum_b_in_ref[n] += fold(pre)
-            pre_round = pre.astype(BF16)
-            pre_ref[n, pl.ds(k * rows, rows), :] = pre_round
-            cot = cot + dot_nt(pre_round, w_in_ref[n])
-        cot_ref[...] = cot
         return carry
 
-    lax.fori_loop(0, steps, backward, 0)
-
-    def gradients(n, carry):
-        grads_ref[n, :width, :] = dot(xt_ref[...], pre_ref[n])
-        grads_ref[n, width : 2 * width, :] = dot(ut_ref[...], act_ref[n]).T
-        return carry
-
-    lax.fori_loop(0, chunks, gradients, 0)
-
-    dec_grad = jnp.zeros((width, 2 * seen_width), F32)
-    dec_grad = dec_grad + dot(xt_ref[:, rows:], miss_ref[: (steps - 1) * rows, :])
+    lax.fori_loop(0, steps, backward, 0, unroll=UNROLL_B)
+
+    for n in range(chunks):
+        part = pl.ds(n * width, width)
+        grads_ref[n, :width, :] = dot(xt_ref[...], pre_ref[:, part])
+        grads_ref[n, width : 2 * width, :] = dot(ut_ref[...], act_ref[:, part]).T
+    dec_grad = dot(xt_ref[:, rows:], miss_ref[rows : steps * rows, :])
     last = lax.dot_general(
         x_ref[steps],
-        miss_ref[(steps - 1) * rows :, :],
+        miss_ref[steps * rows :, :],
         (((0,), (0,)), ((), ())),
         preferred_element_type=F32,
     )
@@ -184,7 +205,7 @@
         ]
         grads_ref[n, tail:line, :] = jnp.concatenate(pieces, axis=1)
         grads_ref[n, line:, :] = jnp.zeros((grads_ref.shape[1] - line, width), F32)
-        grads_ref[n, line : line + 1, :] = jnp.sum(sum_b_in_ref[n], axis=0, keepdims=True)
+        grads_ref[n, line : line + 1, :] = jnp.sum(sum_b_in_ref[:, n * width : (n + 1) * width], axis=0, keepdims=True)
         grads_ref[n, line + 1 : line + 2, :] = jnp.sum(
             sum_b_out_ref[...], axis=0, keepdims=True
         )
@@ -229,8 +250,8 @@
         pltpu.VMEM((steps + 1, rows, width), BF16),
         pltpu.VMEM((width, steps * rows), BF16),
         pltpu.VMEM((width, steps * rows), BF16),
-        pltpu.VMEM((chunks, steps * rows, width), BF16),
-        pltpu.VMEM((chunks, steps * rows, width), BF16),
+        pltpu.VMEM((steps * rows, chunks * width), BF16),
+        pltpu.VMEM((steps * rows, chunks * width), BF16),
         pltpu.VMEM((steps, rows, width), F32),
         pltpu.VMEM((seen_count, rows, seen_width), F32),
         pltpu.VMEM((seen_count, rows, rows), jnp.int32),
@@ -239,10 +260,15 @@
         pltpu.VMEM((rows, rows), jnp.int32),
         pltpu.VMEM((rows, width), F32),
         pltpu.VMEM((rows, width), F32),
-        pltpu.VMEM((chunks, 8, width), F32),
+        pltpu.VMEM((8, chunks * width), F32),
         pltpu.VMEM((8, width), F32),
-        pltpu.VMEM((steps * rows, 2 * seen_width), BF16),
+        pltpu.VMEM(((steps + 1) * rows, 2 * seen_width), BF16),
         pltpu.VMEM((rows * seen_count, seen_width), F32),
+        pltpu.VMEM((chunks * width, width), BF16),
+        pltpu.VMEM((width, chunks * width), BF16),
+        pltpu.VMEM((2 * seen_width, width), BF16),
+        pltpu.VMEM((width, chunks * width), BF16),
+        pltpu.VMEM((1, chunks * width), F32),
     ]
     scratch += [pltpu.VMEM(operands[i].shape, operands[i].dtype) for i in loaded]
     scratch += [pltpu.SemaphoreType.DMA((len(loaded),))]

time: 106 us -> 94.8 us (0.89)
  Pallas kernels: 98.9 us -> 87.6 us
    pallas_call x1, Pallas kernels: 49.6 us -> 38.3 us  [core(): pl.pallas_call(body, out_shape=out, in_specs=specs, out_specs=[vmem] * 3,...]
where the time goes in v1:
time: 94.8 us; the launch traced here: 94.6 us
  Pallas kernels  87.6 us (92%)
  local copies, waits for them, and re-layouts  6.32 us (7%)
    pallas_call x1, Pallas kernels, core(): pl.pallas_call(body, out_shape=out, in_specs=specs, out_specs=[vmem] * 3,...  38.3 us
    pallas_call x1, Pallas kernels, reduce_all(): pl.pallas_call(body, out_shape=[jax.ShapeDtypeStruct((grad_rows, width),...  37.2 us
    pallas_call x1, Pallas kernels, gather(): pl.pallas_call(gather_kernel, out_shape=[jax.ShapeDtypeStruct((count,) +...  11.2 us
    unnamed x12, local copies, waits for them, and re-layouts  5.66 us

profile of v1, /device:TPU:0, one launch (start us, length us, event | category | flops | bytes accessed | tf_op | source)
XLA Modules:
  0.0 94.6 jit_solution(2683504734169050011)
XLA Ops:
  0.6 0.7 broadcast_in_dim.20.b_in_ref
  1.3 0.0 copy-start.1
  1.3 0.9 copy-done.1
  2.2 0.0 copy-start.2
  2.2 0.9 copy-done.2
  3.1 11.2 %gather_weights.1 = (bf16[4,256,256]{2,1,0:T(8,128)(2,1)S(1)}, bf16[4,256,256]{2,1,0:T(8,128)(2,1)S(1)}, f32[4,8,256]{2,1,0:T(8,128)S(1)}) custom-call(bf16[256,256]{1,0:T(8,128)(2,1)S(1)} %copy-done.1, bf16[256,256]{1,0:T(8,128)(2,1)S(1)} %copy-done.2, bf16[1,256]{1,0:T(2,128)(2,1)S(1)} %broadcast_in_dim.20.b_in_ref), custom_call_target="tpu_custom_call" | custom-call | bytes 33554432 | tf_op jit(solution)/shard_map/gather_weights/pallas_call | solution.py:352
  14.3 0.0 copy-start.3
  14.3 0.8 copy-done.3
  15.1 0.0 copy-start.4
  15.1 0.8 copy-done.4
  15.9 0.0 copy-start.5
  15.9 0.6 copy-done.5
  16.5 38.3 %sde.1 = (f32[1,128]{1,0:T(1,128)}, f32[4,576,256]{2,1,0:T(8,128)}, f32[128,256]{1,0:T(8,128)}) custom-call(f32[128,256]{1,0:T(8,128)} %refs_0_.1, bf16[32,128,256]{2,1,0:T(8,128)(2,1)} %refs_1_.1, f32[1,128]{1,0:T(1,128)} %bitcast.16, s32[1,128]{1,0:T(1,128)} %bitcast.17, s32[8,128]{1,0:T(8,128)} %bitcast.10, bf16[128,8,128]{2,1,0:T(8,128)(2,1)} %refs_5_.1, ...), custom_call_target="tpu_custom_call" | custom-call | flops 12884901888 | bytes 8388608 | tf_op jit(solution)/shard_map/sde/pallas_call | solution.py:275
  54.8 0.0 copy-start
  54.8 1.7 %copy-done = f32[4,576,256]{2,1,0:T(8,128)S(1)} copy-done((f32[4,576,256]{2,1,0:T(8,128)S(1)}, f32[4,576,256]{2,1,0:T(8,128)}, u32[]{:S(2)}) %copy-start) | copy-done | bytes 2359320
  56.5 37.2 %reduce_grads.1 = (f32[576,256]{1,0:T(8,128)S(1)}, f32[4,32,256]{2,1,0:T(8,128)S(1)}) custom-call(f32[4,576,256]{2,1,0:T(8,128)S(1)} %copy-done), custom_call_target="tpu_custom_call" | custom-call | tf_op jit(solution)/shard_map/reduce_grads/pallas_call | solution.py:551
  93.7 0.9 finish.1
Async XLA Ops:
  1.3 0.9 copy-start.1
  2.2 0.9 copy-start.2
  14.3 0.8 copy-start.3
  15.1 0.8 copy-start.4
  15.9 0.6 copy-start.5
  54.8 1.7 %copy-start = (f32[4,576,256]{2,1,0:T(8,128)S(1)}, f32[4,576,256]{2,1,0:T(8,128)}, u32[]{:S(2)}) copy-start(f32[4,576,256]{2,1,0:T(8,128)} %get-tuple-element.26.refs_0_) | copy-start | bytes 7077892

commit v2 on v0

v2 whole, which is shorter than its diff:
```python
import jax
import jax.numpy as jnp
from jax import lax
from jax.experimental import pallas as pl
from jax.experimental.pallas import tpu as pltpu
from jax.sharding import PartitionSpec as P

F32 = jnp.float32
BF16 = jnp.bfloat16
UNITS = (0, 1)
UNROLL = 2


def fold(value):
    return value.reshape(-1, 8, value.shape[1]).sum(axis=0)


def send(source, target, sems, index, peer):
    return pltpu.make_async_remote_copy(
        src_ref=source,
        dst_ref=target,
        send_sem=sems[0].at[index],
        recv_sem=sems[1].at[index],
        device_id=peer,
        device_id_type=pl.DeviceIdType.MESH,
    )


def push(value, slot, unit):
    pltpu.matmul_push_rhs(value, slot, unit)


def multiply(acc, value, slot):
    pltpu.matmul_acc_lhs(acc, value, load_staged_rhs=slot)


class Refs:
    def __init__(self, names, refs):
        for name, ref in zip(names, refs, strict=True):
            setattr(self, name, ref)


def train_kernel(r, members, total_rows):
    rows, width = r.init.shape
    steps = r.noise.shape[0]
    seen_count = r.obs.shape[0]
    seen_width = r.dec.shape[1]
    chunks = r.w_in.shape[0]
    first, second, third, aside, wide = r.first, r.second, r.third, r.aside, r.wide

    mine = lax.axis_index("mp")
    batch = lax.axis_index("batch")
    chip, unit = mine // 2, mine % 2
    sibling = chip * 2 + (1 - unit)
    across = (1 - chip) * 2 + unit
    diagonal = (1 - chip) * 2 + (1 - unit)
    to_sibling, to_across, to_diagonal = (batch, sibling), (batch, across), (batch, diagonal)
    group = (to_sibling, to_across, to_diagonal)
    group_at = (sibling, across, diagonal)
    others_at = [lax.rem(batch + d, members) for d in range(1, members)]
    others = [(at, mine) for at in others_at]
    origins = [lax.rem(batch + members - d, members) for d in range(1, members)]

    loads = {}
    for i, (name, source, target) in enumerate(
        (
            ("w_in", r.w_in_own, r.w_in.at[mine]),
            ("b_in", r.b_in_own, r.b_in_flat),
            ("w_out", r.w_out_own, r.w_out.at[mine]),
            ("step", r.step_hbm, r.step),
            ("length", r.length_hbm, r.length),
            ("obs", r.obs_hbm, r.obs),
            ("init", r.init_hbm, r.init),
            ("b_out", r.b_out_hbm, r.b_out),
            ("dec", r.dec_hbm, r.dec),
            ("rate", r.rate_hbm, r.rate),
            ("diff", r.diff_hbm, r.diff),
            ("noise", r.noise_hbm, r.noise),
            ("seen", r.seen_hbm, r.seen),
        )
    ):
        loads[name] = pltpu.make_async_copy(source, target, r.load_sem.at[i])
        loads[name].start()

    barrier = pltpu.get_barrier_semaphore()
    for peer in list(group) + others:
        pl.semaphore_signal(barrier, inc=1, device_id=peer, device_id_type=pl.DeviceIdType.MESH)
    loads["b_in"].wait()
    r.bias_own[...] = jnp.broadcast_to(
        r.b_in_flat[...].astype(F32).reshape(1, width), r.bias_own.shape
    )
    pl.semaphore_wait(barrier, len(group) + len(others))

    whole = (r.w_in, r.bias, r.w_out)
    own = (r.w_in.at[mine], r.bias_own, r.w_out.at[mine])
    loads["w_in"].wait()
    far, near = [None] * 3, [None] * 3
    for i in (0, 1, 2):
        if i == 2:
            loads["w_out"].wait()
        far[i] = send(own[i], whole[i].at[mine], r.far_sem, i, to_across)
        far[i].start()
        near[i] = send(own[i], whole[i].at[mine], r.near_sem, i, to_sibling)
        near[i].start()
    r.bias[mine] = r.bias_own[...]

    def column(row):
        return jnp.broadcast_to(row, (rows, rows)).T

    for name in ("step", "length", "obs", "init", "b_out", "dec", "rate", "diff"):
        loads[name].wait()
    r.dt[...] = column(r.step[...])
    r.root[...] = jnp.sqrt(r.dt[...])
    r.len_wide[...] = column(r.length[...])
    for j in range(seen_count):
        wide_obs = column(r.obs[j : j + 1, :])
        r.obs_wide[j] = wide_obs
        r.obs_half[j] = wide_obs.astype(F32).astype(BF16)
    r.picked[...] = jnp.zeros_like(r.picked)
    r.kl[...] = jnp.zeros_like(r.kl)
    r.sum_b_in[...] = jnp.zeros_like(r.sum_b_in)
    r.sum_b_out[...] = jnp.zeros_like(r.sum_b_out)
    r.state[...] = r.init[...]
    r.x[0] = r.init[...].astype(BF16)
    r.dec_wide[:, :seen_width] = r.dec[...]
    r.dec_wide[:, seen_width:] = jnp.zeros((width, width - seen_width), BF16)
    dec_t = r.dec[...].T
    r.dec_t[:seen_width, :] = dec_t
    r.dec_t[seen_width:, :] = dec_t
    for u in UNITS:
        for acc in (first[u], second[u], third[u], wide[u]):
            pltpu.matmul_pop(acc)
    pltpu.matmul_pop(aside)

    relayed = []
    for i in (0, 1, 2):
        far[i].wait_recv()
        at = whole[i].at[across]
        copy = send(at, at, r.relay_sem, i, to_sibling)
        copy.start()
        relayed.append(copy)
    loads["noise"].wait()
    loads["seen"].wait()
    r.target[...] = r.seen[...].astype(F32).reshape(r.target.shape)
    for copy in far:
        copy.wait_send()
    for copy in near + relayed:
        copy.wait()

    pair = len(UNITS)
    halves = chunks // pair

    def tile(n):
        return slice(n * width, (n + 1) * width)

    def both(value):
        return jnp.concatenate([value] * (width // rows), axis=1)

    for n in range(chunks):
        r.bias_row[:, tile(n)] = r.bias[n, :1, :]

    def stage_pair(read):
        for slot in range(halves):
            for u in UNITS:
                push(read(slot * pair + u), slot, u)

    def discharge():
        for u in UNITS:
            for slot, acc in ((0, first[u]), (1, second[u])):
                multiply(acc, r.x[0], slot)
                pltpu.matmul_pop(acc)

    def two_phases(x, side, between, later, upcoming):
        for u in UNITS:
            multiply(first[u], x, 0)
        if side is not None:
            push(side[1], 0, 0)
            push(later(1), 0, 1)
        else:
            for u in UNITS:
                push(later(u), 0, u)
        for u in UNITS:
            multiply(second[u], x, 1)
        for u in UNITS:
            push(later(pair + u), 1, u)
        if side is not None:
            multiply(aside, side[0], 0)
            push(later(0), 0, 0)
        for u in UNITS:
            multiply(third[u], between(u, pltpu.matmul_pop(first[u])), 0)
        for u in UNITS:
            push(upcoming(u), 0, u)
        for u in UNITS:
            multiply(third[u], between(pair + u, pltpu.matmul_pop(second[u])), 1)
        for u in UNITS:
            push(upcoming(pair + u), 1, u)
        extra = pltpu.matmul_pop(aside) if side is not None else None
        return pltpu.matmul_pop(third[0]) + pltpu.matmul_pop(third[1]), extra

    def pick(index, x):
        at = jnp.full((1, 1), index, jnp.int32).astype(F32).astype(BF16)
        for j in range(seen_count):
            hit = r.obs_half[j] == at
            for m in range(width // rows):
                lanes = slice(m * rows, (m + 1) * rows)
                r.picked[j, :, lanes] = jnp.where(hit, x[:, lanes], r.picked[j, :, lanes])

    def forward(k, carry):
        x = r.x[k]

        def between(n, raw):
            act = jnp.tanh(raw + r.bias_row[:, tile(n)]).astype(BF16)
            r.act[pl.ds(k * rows, rows), tile(n)] = act
            return act

        total, _ = two_phases(x, None, between, lambda n: r.w_out[n], lambda n: r.w_in[n])
        drift = total + r.b_out[...]
        state = r.state[...]
        inv = 1.0 / r.diff[...]
        live = k < r.len_wide[...]
        factor = both(jnp.where(live, r.dt[...], 0.0))
        root = both(jnp.where(live, r.root[...], 0.0))
        following = state + (factor * drift + r.diff[...] * root * r.noise[k].astype(F32))
        r.state[...] = following
        r.x[k + 1] = following.astype(BF16)
        residual = (drift + r.rate[...] * state) * inv
        r.kl[...] += factor * residual * residual
        r.scaled[k] = residual * inv
        r.xt[:, pl.ds(pl.multiple_of(k * rows, rows), rows)] = x.T
        pick(k, x)
        return carry

    stage_pair(lambda n: r.w_in[n])
    lax.fori_loop(0, steps, forward, 0, unroll=UNROLL)
    discharge()
    pick(steps, r.x[steps])

    square = jnp.zeros((rows, seen_width), F32)
    seen_accs = (first[0], first[1], second[0], second[1])
    for u in UNITS:
        push(r.dec_wide[...], 0, u)
    loaded = [False, False]
    for start in range(0, seen_count, len(seen_accs)):
        batch_j = list(range(start, min(start + len(seen_accs), seen_count)))
        for at, (acc, j) in enumerate(zip(seen_accs, batch_j)):
            u = at % 2
            multiply(acc, r.picked[j], None if loaded[u] else 0)
            loaded[u] = True
        for acc, j in zip(seen_accs, batch_j):
            misfit = (
                pltpu.matmul_pop(acc)[:, :seen_width]
                - r.target[pl.ds(j, rows, stride=seen_count), :]
            )
            square = square + misfit * misfit
            rounded = misfit.astype(BF16)
            r.misfit[j] = rounded.astype(F32)
            r.misfit_wide[j * rows : (j + 1) * rows, :seen_width] = rounded
    r.misfit_wide[:, seen_width:] = jnp.zeros(
        (seen_count * rows, width - seen_width), BF16
    )
    per = width // rows
    for p in range(seen_count // per):
        u = p % 2
        left = jnp.concatenate([r.picked[p * per + m].T for m in range(per)], axis=1)
        push(r.misfit_wide[p * width : (p + 1) * width, :], 0, u)
        multiply(wide[u], left, 0)
    dec_grad = (pltpu.matmul_pop(wide[0]) + pltpu.matmul_pop(wide[1]))[:, :seen_width]
    loglik = -0.5 * jnp.sum(square.T, axis=0, keepdims=True)
    kl_half = r.kl[:, :rows]
    for part in range(1, width // rows):
        kl_half = kl_half + r.kl[:, part * rows : (part + 1) * rows]
    kl_row = 0.5 * jnp.sum(kl_half.T, axis=0, keepdims=True)
    divisor = (width * r.length[...] + seen_width * seen_count).astype(F32)
    r.elbo[...] = (loglik - kl_row) / divisor

    quarter = width // chunks
    score_rows = jnp.concatenate(
        [loglik, kl_row, jnp.zeros((6, rows), F32)], axis=0
    )
    for n in range(chunks):
        r.dec_part[n, :quarter, :] = dec_grad[n * quarter : (n + 1) * quarter, :]
        r.dec_part[n, quarter:, :] = score_rows
    dec_first = []
    for i, (peer, at) in enumerate(zip(group, group_at)):
        copy = send(r.dec_part.at[at], r.dec_got.at[i], r.dec_sem, i, peer)
        copy.start()
        dec_first.append(copy)

    for n in range(chunks):
        r.w_in_t[n] = r.w_in[n].T
        r.w_out_t[n] = r.w_out[n].T

    def obs_sum(index):
        total = jnp.zeros((rows, seen_width), F32)
        for j in range(seen_count):
            total = total + jnp.where(r.obs_wide[j] == index, r.misfit[j], 0.0)
        high = total.astype(BF16)
        low = (total - high.astype(F32)).astype(BF16)
        return jnp.concatenate([high, low], axis=1)

    push(r.dec_t[...], 0, 0)
    multiply(aside, obs_sum(steps), 0)
    r.cot[...] = pltpu.matmul_pop(aside)
    stage_pair(lambda n: r.w_out_t[n])

    def backward(index, carry):
        k = steps - 1 - index
        cot = r.cot[...]
        scaled = r.scaled[k]
        factor = both(jnp.where(k < r.len_wide[...], r.dt[...], 0.0))
        update = factor * (cot + scaled)
        rounded = update.astype(BF16)

        def between(n, raw):
            act = r.act[pl.ds(k * rows, rows), tile(n)].astype(F32)
            pre = raw * (1.0 - act * act)
            pre_round = pre.astype(BF16)
            r.pre[pl.ds(k * rows, rows), tile(n)] = pre_round
            r.sum_b_in[:, tile(n)] += fold(pre)
            return pre_round

        total, seen_back = two_phases(
            rounded,
            (obs_sum(k), r.dec_t[...]),
            between,
            lambda n: r.w_in_t[n],
            lambda n: r.w_out_t[n],
        )
        r.cot[...] = total + (cot + factor * r.rate[...] * scaled + seen_back)
        r.ut[:, pl.ds(pl.multiple_of(k * rows, rows), rows)] = rounded.T
        r.sum_b_out[...] += fold(update)
        return carry

    cut_a, cut_b = steps * 3 // 8 // 2 * 2, steps * 6 // 8 // 2 * 2
    lax.fori_loop(0, cut_a, backward, 0, unroll=UNROLL)
    for copy in dec_first:
        copy.wait_recv()
    dec_sum = r.dec_part[mine]
    for i in range(len(group)):
        dec_sum = dec_sum + r.dec_got[i]
    r.dec_mid[batch] = dec_sum
    dec_second = []
    for d, peer in enumerate(others):
        copy = send(r.dec_mid.at[batch], r.dec_mid.at[batch], r.dec_all_sem, d, peer)
        copy.start()
        dec_second.append(copy)
    lax.fori_loop(cut_a, cut_b, backward, 0, unroll=UNROLL)
    for d, origin in enumerate(origins):
        send(
            r.dec_mid.at[origin], r.dec_mid.at[origin], r.dec_all_sem, d, (origin, mine)
        ).wait_recv()
    dec_total = r.dec_mid[0]
    for b in range(1, members):
        dec_total = dec_total + r.dec_mid[b]
    r.decs[mine] = dec_total / total_rows
    dec_third = []
    for i, peer in enumerate(group):
        copy = send(r.decs.at[mine], r.decs.at[mine], r.dec_out_sem, i, peer)
        copy.start()
        dec_third.append(copy)
    lax.fori_loop(cut_b, steps, backward, 0, unroll=UNROLL)
    discharge()

    b_out_sum = jnp.sum(r.sum_b_out[...], axis=0, keepdims=True)
    pad = jnp.zeros((6, width), F32)
    for n in range(chunks):
        b_in_sum = jnp.sum(r.sum_b_in[:, tile(n)], axis=0, keepdims=True)
        r.b_part[n] = jnp.concatenate([b_in_sum, b_out_sum, pad], axis=0)
    r.b_got[mine] = r.b_part[mine]
    b_first = []
    for i, (peer, at) in enumerate(zip(group, group_at)):
        copy = send(r.b_part.at[at], r.b_got.at[mine], r.b_sem, i, peer)
        copy.start()
        b_first.append(copy)

    depth = width
    parts = steps * rows // depth
    sources = ((r.xt, r.pre), (r.ut, r.act))

    def products(t, quarters):
        left_ref, right_ref = sources[t]
        for p in range(parts):
            k_rows = slice(p * depth, (p + 1) * depth)
            for u, n in zip(UNITS, quarters):
                lanes = pl.ds(pl.multiple_of(n * width, width), width)
                push(right_ref[k_rows, lanes], p % 2, u)
                multiply(wide[u], left_ref[:, k_rows], p % 2)
        return [pltpu.matmul_pop(wide[u]) for u in UNITS]

    near_copies = []

    def exchange(t):
        for i, quarters in enumerate(((diagonal, across), (sibling, mine))):
            away, keep = products(t, quarters)
            r.near_out[t, i] = away
            copy = send(
                r.near_out.at[t, i], r.near_in.at[t, i], r.grad_sem, 2 * t + i, to_sibling
            )
            copy.start()
            near_copies.append(copy)
            r.keep[t, i] = keep

    far_copies = []

    def cross(t):
        near_copies[2 * t].wait_recv()
        r.far_out[t] = (r.keep[t, 0] + r.near_in[t, 0]).astype(BF16)
        copy = send(r.far_out.at[t], r.far_in.at[t], r.cross_sem, t, to_across)
        copy.start()
        far_copies.append(copy)

    piece = width // members
    scatter_copies = [[], []]

    def scatter(t):
        near_copies[2 * t + 1].wait_recv()
        far_copies[t].wait_recv()
        full = r.keep[t, 1] + r.near_in[t, 1] + r.far_in[t].astype(F32)
        r.full[t] = full.reshape(members, piece, width)
        r.scatter_out[t] = full.astype(BF16).reshape(members, piece, width)
        for d, (peer, at) in enumerate(zip(others, others_at)):
            copy = send(
                r.scatter_out.at[t, at],
                r.scatter_in.at[t, d],
                r.scatter_sem,
                t * (members - 1) + d,
                peer,
            )
            copy.start()
            scatter_copies[t].append(copy)

    spread_copies = []

    def spread(t):
        value = r.full[t, batch]
        for d in range(members - 1):
            scatter_copies[t][d].wait_recv()
            value = value + r.scatter_in[t, d].astype(F32)
        r.done[t, batch] = (value / total_rows).astype(BF16)
        for d, peer in enumerate(others):
            copy = send(
                r.done.at[t, batch],
                r.done.at[t, batch],
                r.spread_sem,
                t * (members - 1) + d,
                peer,
            )
            copy.start()
            spread_copies.append(copy)

    def collect(t):
        for d, origin in enumerate(origins):
            send(
                r.done.at[t, origin],
                r.done.at[t, origin],
                r.spread_sem,
                t * (members - 1) + d,
                (origin, mine),
            ).wait_recv()

    exchange(0)
    cross(0)
    exchange(1)
    cross(1)
    for i, (peer, at) in enumerate(zip(group, group_at)):
        send(r.b_part.at[at], r.b_got.at[at], r.b_sem, i, peer).wait_recv()
    b_sum = r.b_got[0]
    for n in range(1, chunks):
        b_sum = b_sum + r.b_got[n]
    r.b_mid[batch] = b_sum
    b_second = []
    for d, peer in enumerate(others):
        copy = send(r.b_mid.at[batch], r.b_mid.at[batch], r.b_all_sem, d, peer)
        copy.start()
        b_second.append(copy)
    scatter(0)
    scatter(1)
    spread(0)
    spread(1)
    for i, (peer, at) in enumerate(zip(group, group_at)):
        send(r.decs.at[at], r.decs.at[at], r.dec_out_sem, i, peer).wait_recv()
    for d, origin in enumerate(origins):
        send(
            r.b_mid.at[origin], r.b_mid.at[origin], r.b_all_sem, d, (origin, mine)
        ).wait_recv()
    b_total = r.b_mid[0]
    for b in range(1, members):
        b_total = b_total + r.b_mid[b]
    r.b_done[...] = b_total / total_rows
    for copy in (
        dec_first + dec_second + dec_third + b_first + b_second + near_copies + far_copies
    ):
        copy.wait_send()
    for copy in scatter_copies[0] + scatter_copies[1]:
        copy.wait_send()
    collect(0)
    collect(1)
    for copy in spread_copies:
        copy.wait_send()


def finish_kernel(
    done_ref,
    b_ref,
    decs_ref,
    cot_ref,
    elbo_ref,
    w_in_out,
    w_out_out,
    b_in_out,
    b_out_out,
    dec_out,
    scores_out,
    cot_out,
    elbo_out,
):
    _, members, piece, width = done_ref.shape
    for b in range(members):
        part = slice(b * piece, (b + 1) * piece)
        w_in_out[part, :] = done_ref[0, b].astype(F32)
    w_out_out[...] = done_ref[1].astype(F32).reshape(members * piece, width).T
    b_in_out[...] = b_ref[0:1, :]
    b_out_out[...] = b_ref[1:2, :]
    quarter = dec_out.shape[0] // decs_ref.shape[0]
    for n in range(decs_ref.shape[0]):
        dec_out[n * quarter : (n + 1) * quarter, :] = decs_ref[n, :quarter, :]
    likelihood = jnp.zeros((1, 1), F32)
    divergence = jnp.zeros((1, 1), F32)
    for n in range(decs_ref.shape[0]):
        share = decs_ref[n, quarter : quarter + 2, :]
        likelihood = share[0:1] if n == 0 else likelihood
        divergence = share[1:2] if n == 0 else divergence
    scores_out[:, 0:1] = jnp.sum(likelihood, axis=1, keepdims=True)
    scores_out[:, 1:2] = jnp.sum(divergence, axis=1, keepdims=True)
    cot_out[...] = cot_ref[...]
    elbo_out[...] = elbo_ref[...]


def on_device(
    init_state,
    brownian,
    step_size,
    lengths,
    obs_steps,
    observed,
    w_in,
    b_in,
    w_out,
    b_out,
    decoder,
    prior_rate,
    diffusion,
):
    rows, width = init_state.shape
    steps = brownian.shape[0]
    seen_count, seen_width = observed.shape[1:]
    chunks, members = lax.axis_size("mp"), lax.axis_size("batch")
    quarter = width // chunks
    piece = width // members
    total_rows = rows * chunks * members
    hidden = chunks * width
    hbm = pl.BlockSpec(memory_space=pltpu.HBM)
    vmem = pl.BlockSpec(memory_space=pltpu.VMEM)

    inputs = {
        "init_hbm": init_state,
        "noise_hbm": brownian,
        "step_hbm": step_size[None, :],
        "length_hbm": lengths[None, :],
        "obs_hbm": obs_steps.T,
        "seen_hbm": observed,
        "w_in_own": w_in,
        "b_in_own": b_in,
        "w_out_own": w_out,
        "b_out_hbm": b_out[None, :],
        "dec_hbm": decoder,
        "rate_hbm": prior_rate[None, :],
        "diff_hbm": diffusion[None, :],
    }
    outputs = {
        "done": ((2, members, piece, width), BF16),
        "b_done": ((8, width), F32),
        "decs": ((chunks, quarter + 8, seen_width), F32),
        "cot": ((rows, width), F32),
        "elbo": ((1, rows), F32),
    }
    scratch = {
        "init": ((rows, width), F32),
        "noise": ((steps, rows, width), BF16),
        "step": ((1, rows), F32),
        "length": ((1, rows), jnp.int32),
        "obs": ((seen_count, rows), jnp.int32),
        "seen": ((rows, seen_count, seen_width), BF16),
        "w_in": ((chunks, width, width), BF16),
        "w_out": ((chunks, width, width), BF16),
        "b_in_flat": ((width,), BF16),
        "bias_own": ((8, width), F32),
        "bias": ((chunks, 8, width), F32),
        "bias_row": ((1, hidden), F32),
        "b_out": ((1, width), F32),
        "dec": ((width, seen_width), BF16),
        "rate": ((1, width), F32),
        "diff": ((1, width), F32),
        "w_in_t": ((chunks, width, width), BF16),
        "w_out_t": ((chunks, width, width), BF16),
        "dec_wide": ((width, width), BF16),
        "dec_t": ((2 * seen_width, width), BF16),
        "dt": ((rows, rows), F32),
        "root": ((rows, rows), F32),
        "len_wide": ((rows, rows), jnp.int32),
        "obs_wide": ((seen_count, rows, rows), jnp.int32),
        "obs_half": ((seen_count, rows, rows), BF16),
        "picked": ((seen_count, rows, width), BF16),
        "misfit": ((seen_count, rows, seen_width), F32),
        "misfit_wide": ((seen_count * rows, width), BF16),
        "target": ((rows * seen_count, seen_width), F32),
        "state": ((rows, width), F32),
        "kl": ((rows, width), F32),
        "sum_b_in": ((8, hidden), F32),
        "sum_b_out": ((8, width), F32),
        "x": ((steps + 1, rows, width), BF16),
        "xt": ((width, steps * rows), BF16),
        "ut": ((width, steps * rows), BF16),
        "act": ((steps * rows, hidden), BF16),
        "pre": ((steps * rows, hidden), BF16),
        "scaled": ((steps, rows, width), F32),
        "dec_part": ((chunks, quarter + 8, seen_width), F32),
        "dec_got": ((3, quarter + 8, seen_width), F32),
        "dec_mid": ((members, quarter + 8, seen_width), F32),
        "b_part": ((chunks, 8, width), F32),
        "b_got": ((chunks, 8, width), F32),
        "b_mid": ((members, 8, width), F32),
        "near_out": ((2, 2, width, width), F32),
        "near_in": ((2, 2, width, width), F32),
        "keep": ((2, 2, width, width), F32),
        "far_out": ((2, width, width), BF16),
        "far_in": ((2, width, width), BF16),
        "full": ((2, members, piece, width), F32),
        "scatter_out": ((2, members, piece, width), BF16),
        "scatter_in": ((2, members - 1, piece, width), BF16),
    }
    waits = {
        "far_sem": 3,
        "near_sem": 3,
        "relay_sem": 3,
        "dec_sem": 3,
        "dec_all_sem": members - 1,
        "dec_out_sem": 3,
        "b_sem": 3,
        "b_all_sem": members - 1,
        "grad_sem": 4,
        "cross_sem": 2,
        "scatter_sem": 2 * (members - 1),
        "spread_sem": 2 * (members - 1),
    }

    def body(*refs):
        refs = list(refs)
        named = Refs(
            list(inputs) + list(outputs) + list(scratch),
            refs[: len(inputs) + len(outputs) + len(scratch)],
        )
        sems = refs[len(inputs) + len(outputs) + len(scratch) :]
        named.load_sem = sems.pop(0)
        for name in waits:
            setattr(named, name, (sems.pop(0), sems.pop(0)))

        def with_accs(*accs):
            named.first, named.second, named.third = accs[0:2], accs[2:4], accs[4:6]
            named.wide, named.aside = accs[6:8], accs[8]
            train_kernel(named, members, total_rows)

        pl.run_scoped(
            with_accs,
            *[pltpu.ACC(u)((rows, width), F32) for _ in range(3) for u in UNITS],
            *[pltpu.ACC(u)((width, width), F32) for u in UNITS],
            pltpu.ACC(0)((rows, width), F32),
        )

    sem_shapes = [pltpu.SemaphoreType.DMA((len(inputs),))]
    for count in waits.values():
        sem_shapes += [pltpu.SemaphoreType.DMA((count,))] * 2
    done, b_done, decs, cot, elbo = pl.pallas_call(
        body,
        out_shape=[jax.ShapeDtypeStruct(*s) for s in outputs.values()],
        in_specs=[hbm] * len(inputs),
        out_specs=[vmem] * len(outputs),
        scratch_shapes=[pltpu.VMEM(*s) for s in scratch.values()] + sem_shapes,
        compiler_params=pltpu.CompilerParams(
            collective_id=0, has_side_effects=True, vmem_limit_bytes=58 * 1024 * 1024
        ),
        name="train",
    )(*inputs.values())
    results = pl.pallas_call(
        finish_kernel,
        out_shape=[
            jax.ShapeDtypeStruct((width, width), F32),
            jax.ShapeDtypeStruct((width, width), F32),
            jax.ShapeDtypeStruct((1, width), F32),
            jax.ShapeDtypeStruct((1, width), F32),
            jax.ShapeDtypeStruct((width, seen_width), F32),
            jax.ShapeDtypeStruct((1, 2), F32),
            jax.ShapeDtypeStruct((rows, width), F32),
            jax.ShapeDtypeStruct((1, rows), F32),
        ],
        in_specs=[vmem] * 5,
        out_specs=[vmem] * 8,
        compiler_params=pltpu.CompilerParams(vmem_limit_bytes=4 * 1024 * 1024),
        name="finish",
    )(done, b_done, decs, cot, elbo)
    own_w_in, own_w_out, own_b_in, b_out_grad, dec_grad, scores, grad_init, elbo = results
    return (
        elbo[0],
        scores[0],
        own_w_in,
        own_b_in[0],
        own_w_out,
        b_out_grad[0],
        dec_grad,
        grad_init,
    )


def solution(mesh):
    both = ("batch", "mp")
    placed = (
        P(both, None),
        P(None, both, None),
        P(both),
        P(both),
        P(both, None),
        P(both, None, None),
        P(None, "mp"),
        P("mp"),
        P("mp", None),
        P(),
        P(),
        P(),
        P(),
    )
    return jax.shard_map(
        on_device,
        mesh=mesh,
        in_specs=placed,
        out_specs=(
            P(both),
            P(),
            P(None, "mp"),
            P("mp"),
            P("mp", None),
            P(),
            P(),
            P(both, None),
        ),
        check_vma=False,
    )
```

time: 106 us -> 73 us (0.69)
  Pallas kernels: 98.9 us -> 68 us
  local copies, waits for them, and re-layouts: 6.32 us -> 4.11 us
    pallas_call x4 -> x2, Pallas kernels: 98.9 us -> 68 us  [the longest x1 67 us: on_device(): pl.pallas_call(body, out_shape=[jax.ShapeDtypeStruct(*s) for s in outputs...]
    unnamed x12 -> x10, local copies, waits for them, and re-layouts: 5.66 us -> 4.11 us
where the time goes in v2:
time: 73 us; the launch traced here: 72.7 us
  Pallas kernels  68 us (93%)
  local copies, waits for them, and re-layouts  4.11 us (6%)
    pallas_call x1, Pallas kernels, on_device(): pl.pallas_call(body, out_shape=[jax.ShapeDtypeStruct(*s) for s in outputs...  67 us
    unnamed x10, local copies, waits for them, and re-layouts  4.11 us

profile of v2, /device:TPU:0, one launch (start us, length us, event | category | flops | bytes accessed | tf_op | source)
XLA Modules:
  0.0 72.7 jit_solution(9857479554793289841)
XLA Ops:
  0.6 67.0 %train.1 = (bf16[2,8,32,256]{3,2,1,0:T(8,128)(2,1)}, f32[8,256]{1,0:T(8,128)}, f32[4,72,128]{2,1,0:T(8,128)}, f32[128,256]{1,0:T(8,128)}, f32[1,128]{1,0:T(1,128)}) custom-call(f32[128,256]{1,0:T(8,128)} %refs_0_.1, bf16[32,128,256]{2,1,0:T(8,128)(2,1)} %refs_1_.1, f32[1,128]{1,0:T(1,128)} %bitcast.14, s32[1,128]{1,0:T(1,128)} %bitcast.15, ...), custom_call_target="tpu_custom_call" | custom-call | tf_op jit(solution)/shard_map/train/pallas_call | solution.py:683
  67.7 0.0 copy-start
  67.7 0.9 %copy-done = bf16[2,8,32,256]{3,2,1,0:T(8,128)(2,1)S(1)} copy-done((bf16[2,8,32,256]{3,2,1,0:T(8,128)(2,1)S(1)}, bf16[2,8,32,256]{3,2,1,0:T(8,128)(2,1)}, u32[]{:S(2)}) %copy-start) | copy-done | bytes 262168
  68.6 0.0 copy-start.1
  68.6 0.9 %copy-done.1 = f32[4,72,128]{2,1,0:T(8,128)S(1)} copy-done((f32[4,72,128]{2,1,0:T(8,128)S(1)}, f32[4,72,128]{2,1,0:T(8,128)}, u32[]{:S(2)}) %copy-start.1) | copy-done | bytes 147480
  69.5 0.0 copy-start.2
  69.5 0.9 %copy-done.2 = f32[128,256]{1,0:T(8,128)S(1)} copy-done((f32[128,256]{1,0:T(8,128)S(1)}, f32[128,256]{1,0:T(8,128)}, u32[]{:S(2)}) %copy-start.2) | copy-done | bytes 131096
  70.4 0.0 copy-start.3
  70.4 0.7 copy-done.3
  71.1 0.0 copy-start.4
  71.1 0.7 copy-done.4
  71.8 1.0 %finish.1 = (f32[256,256]{1,0:T(8,128)}, f32[256,256]{1,0:T(8,128)}, f32[1,256]{1,0:T(1,128)}, f32[1,256]{1,0:T(1,128)}, f32[256,128]{1,0:T(8,128)}, /*index=5*/...) custom-call(bf16[2,8,32,256]{3,2,1,0:T(8,128)(2,1)S(1)} %copy-done, f32[8,256]{1,0:T(8,128)S(1)} %copy-done.3, ...), custom_call_target="tpu_custom_call" | custom-call | tf_op jit(solution)/shard_map/finish/pallas_call | solution.py:694
Async XLA Ops:
  67.7 1.0 %copy-start = (bf16[2,8,32,256]{3,2,1,0:T(8,128)(2,1)S(1)}, bf16[2,8,32,256]{3,2,1,0:T(8,128)(2,1)}, u32[]{:S(2)}) copy-start(bf16[2,8,32,256]{3,2,1,0:T(8,128)(2,1)} %get-tuple-element.21.done_ref) | copy-start | bytes 786436
  68.6 0.9 %copy-start.1 = (f32[4,72,128]{2,1,0:T(8,128)S(1)}, f32[4,72,128]{2,1,0:T(8,128)}, u32[]{:S(2)}) copy-start(f32[4,72,128]{2,1,0:T(8,128)} %get-tuple-element.23.decs_ref) | copy-start | bytes 442372
  69.5 0.9 %copy-start.2 = (f32[128,256]{1,0:T(8,128)S(1)}, f32[128,256]{1,0:T(8,128)}, u32[]{:S(2)}) copy-start(f32[128,256]{1,0:T(8,128)} %get-tuple-element.24.cot_ref) | copy-start | bytes 393220
  70.4 0.7 copy-start.3
  71.1 0.7 copy-start.4

commit v3 on v2

--- a/solution.py
+++ b/solution.py
@@ -9,6 +9,7 @@
 BF16 = jnp.bfloat16
 UNITS = (0, 1)
 UNROLL = 2
+LIMIT = 48 * 1024 * 1024
 
 
 def fold(value):
@@ -115,8 +116,7 @@
     for j in range(seen_count):
         wide_obs = column(r.obs[j : j + 1, :])
         r.obs_wide[j] = wide_obs
-        r.obs_half[j] = wide_obs.astype(F32).astype(BF16)
-    r.picked[...] = jnp.zeros_like(r.picked)
+        r.obs_half[j] = wide_obs.astype(jnp.int16)
     r.kl[...] = jnp.zeros_like(r.kl)
     r.sum_b_in[...] = jnp.zeros_like(r.sum_b_in)
     r.sum_b_out[...] = jnp.zeros_like(r.sum_b_out)
@@ -197,13 +197,31 @@
         extra = pltpu.matmul_pop(aside) if side is not None else None
         return pltpu.matmul_pop(third[0]) + pltpu.matmul_pop(third[1]), extra
 
-    def pick(index, x):
-        at = jnp.full((1, 1), index, jnp.int32).astype(F32).astype(BF16)
+    band = 16
+
+    def pick_band(b, carry):
+        at = pl.ds(pl.multiple_of(b * band, band), band)
+        wanted = [r.obs_half[j, at, :] for j in range(seen_count)]
+
+        def look(k, found):
+            x = r.x[k, at, :]
+            index = jnp.full((band, rows), k, jnp.int32).astype(jnp.int16)
+            out = []
+            for j in range(seen_count):
+                hit = wanted[j] == index
+                for m in range(width // rows):
+                    at_m = j * (width // rows) + m
+                    out.append(jnp.where(hit, x[:, m * rows : (m + 1) * rows], found[at_m]))
+            return tuple(out)
+
+        blank = jnp.zeros((band, rows), BF16)
+        found = lax.fori_loop(
+            1, steps + 1, look, (blank,) * (seen_count * (width // rows)), unroll=4
+        )
         for j in range(seen_count):
-            hit = r.obs_half[j] == at
             for m in range(width // rows):
-                lanes = slice(m * rows, (m + 1) * rows)
-                r.picked[j, :, lanes] = jnp.where(hit, x[:, lanes], r.picked[j, :, lanes])
+                r.picked[j, at, m * rows : (m + 1) * rows] = found[j * (width // rows) + m]
+        return carry
 
     def forward(k, carry):
         x = r.x[k]
@@ -227,13 +245,12 @@
         r.kl[...] += factor * residual * residual
         r.scaled[k] = residual * inv
         r.xt[:, pl.ds(pl.multiple_of(k * rows, rows), rows)] = x.T
-        pick(k, x)
         return carry
 
     stage_pair(lambda n: r.w_in[n])
     lax.fori_loop(0, steps, forward, 0, unroll=UNROLL)
     discharge()
-    pick(steps, r.x[steps])
+    lax.fori_loop(0, rows // band, pick_band, 0)
 
     square = jnp.zeros((rows, seen_width), F32)
     seen_accs = (first[0], first[1], second[0], second[1])
@@ -331,8 +348,8 @@
         r.sum_b_out[...] += fold(update)
         return carry
 
-    cut_a, cut_b = steps * 3 // 8 // 2 * 2, steps * 6 // 8 // 2 * 2
-    lax.fori_loop(0, cut_a, backward, 0, unroll=UNROLL)
+    cut = steps * 3 // 8 // 2 * 2
+    lax.fori_loop(0, cut, backward, 0, unroll=UNROLL)
     for copy in dec_first:
         copy.wait_recv()
     dec_sum = r.dec_part[mine]
@@ -344,21 +361,7 @@
         copy = send(r.dec_mid.at[batch], r.dec_mid.at[batch], r.dec_all_sem, d, peer)
         copy.start()
         dec_second.append(copy)
-    lax.fori_loop(cut_a, cut_b, backward, 0, unroll=UNROLL)
-    for d, origin in enumerate(origins):
-        send(
-            r.dec_mid.at[origin], r.dec_mid.at[origin], r.dec_all_sem, d, (origin, mine)
-        ).wait_recv()
-    dec_total = r.dec_mid[0]
-    for b in range(1, members):
-        dec_total = dec_total + r.dec_mid[b]
-    r.decs[mine] = dec_total / total_rows
-    dec_third = []
-    for i, peer in enumerate(group):
-        copy = send(r.decs.at[mine], r.decs.at[mine], r.dec_out_sem, i, peer)
-        copy.start()
-        dec_third.append(copy)
-    lax.fori_loop(cut_b, steps, backward, 0, unroll=UNROLL)
+    lax.fori_loop(cut, steps, backward, 0, unroll=UNROLL)
     discharge()
 
     b_out_sum = jnp.sum(r.sum_b_out[...], axis=0, keepdims=True)
@@ -387,33 +390,31 @@
                 multiply(wide[u], left_ref[:, k_rows], p % 2)
         return [pltpu.matmul_pop(wide[u]) for u in UNITS]
 
-    near_copies = []
-
-    def exchange(t):
-        for i, quarters in enumerate(((diagonal, across), (sibling, mine))):
-            away, keep = products(t, quarters)
-            r.near_out[t, i] = away
-            copy = send(
-                r.near_out.at[t, i], r.near_in.at[t, i], r.grad_sem, 2 * t + i, to_sibling
-            )
-            copy.start()
-            near_copies.append(copy)
-            r.keep[t, i] = keep
+    near_copies = {}
+
+    def exchange(t, i):
+        away, keep = products(t, ((diagonal, across), (sibling, mine))[i])
+        r.near_out[t, i] = away
+        copy = send(r.near_out.at[t, i], r.near_in.at[t, i], r.grad_sem, 2 * t + i, to_sibling)
+        copy.start()
+        near_copies[t, i] = copy
+        r.keep[t, i] = keep
 
     far_copies = []
 
     def cross(t):
-        near_copies[2 * t].wait_recv()
+        near_copies[t, 0].wait_recv()
         r.far_out[t] = (r.keep[t, 0] + r.near_in[t, 0]).astype(BF16)
         copy = send(r.far_out.at[t], r.far_in.at[t], r.cross_sem, t, to_across)
         copy.start()
         far_copies.append(copy)
 
     piece = width // members
+    lane = r.scale.shape[3]
     scatter_copies = [[], []]
 
     def scatter(t):
-        near_copies[2 * t + 1].wait_recv()
+        near_copies[t, 1].wait_recv()
         far_copies[t].wait_recv()
         full = r.keep[t, 1] + r.near_in[t, 1] + r.far_in[t].astype(F32)
         r.full[t] = full.reshape(members, piece, width)
@@ -436,7 +437,25 @@
         for d in range(members - 1):
             scatter_copies[t][d].wait_recv()
             value = value + r.scatter_in[t, d].astype(F32)
-        r.done[t, batch] = (value / total_rows).astype(BF16)
+        value = value / total_rows
+        top = jnp.max(jnp.abs(value), axis=0, keepdims=True)
+        share = top[:, :lane]
+        for m in range(1, width // lane):
+            share = jnp.maximum(share, top[:, m * lane : (m + 1) * lane])
+        scale = jnp.maximum(share, 1e-30) * (1.0 / 32767.0)
+        grow = jnp.concatenate([1.0 / scale] * (width // lane), axis=1)
+        r.done[t, batch] = jnp.round(value * grow).astype(jnp.int32).astype(jnp.int16)
+        r.scale[t, batch] = scale
+        for d, peer in enumerate(others):
+            copy = send(
+                r.scale.at[t, batch],
+                r.scale.at[t, batch],
+                r.scale_sem,
+                t * (members - 1) + d,
+                peer,
+            )
+            copy.start()
+            spread_copies.append(copy)
         for d, peer in enumerate(others):
             copy = send(
                 r.done.at[t, batch],
@@ -450,18 +469,29 @@
 
     def collect(t):
         for d, origin in enumerate(origins):
-            send(
-                r.done.at[t, origin],
-                r.done.at[t, origin],
-                r.spread_sem,
-                t * (members - 1) + d,
-                (origin, mine),
-            ).wait_recv()
-
-    exchange(0)
+            for ref, sems in ((r.scale, r.scale_sem), (r.done, r.spread_sem)):
+                at = ref.at[t, origin]
+                send(at, at, sems, t * (members - 1) + d, (origin, mine)).wait_recv()
+
+    exchange(0, 0)
+    exchange(1, 0)
     cross(0)
-    exchange(1)
+    exchange(0, 1)
     cross(1)
+    exchange(1, 1)
+    for d, origin in enumerate(origins):
+        send(
+            r.dec_mid.at[origin], r.dec_mid.at[origin], r.dec_all_sem, d, (origin, mine)
+        ).wait_recv()
+    dec_total = r.dec_mid[0]
+    for b in range(1, members):
+        dec_total = dec_total + r.dec_mid[b]
+    r.decs[mine] = dec_total / total_rows
+    dec_third = []
+    for i, peer in enumerate(group):
+        copy = send(r.decs.at[mine], r.decs.at[mine], r.dec_out_sem, i, peer)
+        copy.start()
+        dec_third.append(copy)
     for i, (peer, at) in enumerate(zip(group, group_at)):
         send(r.b_part.at[at], r.b_got.at[at], r.b_sem, i, peer).wait_recv()
     b_sum = r.b_got[0]
@@ -488,7 +518,7 @@
         b_total = b_total + r.b_mid[b]
     r.b_done[...] = b_total / total_rows
     for copy in (
-        dec_first + dec_second + dec_third + b_first + b_second + near_copies + far_copies
+        dec_first + dec_second + dec_third + b_first + b_second + list(near_copies.values()) + far_copies
     ):
         copy.wait_send()
     for copy in scatter_copies[0] + scatter_copies[1]:
@@ -501,6 +531,7 @@
 
 def finish_kernel(
     done_ref,
+    scale_ref,
     b_ref,
     decs_ref,
     cot_ref,
@@ -515,10 +546,16 @@
     elbo_out,
 ):
     _, members, piece, width = done_ref.shape
+    lane = scale_ref.shape[3]
+
+    def value(t, b):
+        scale = jnp.concatenate([scale_ref[t, b]] * (width // lane), axis=1)
+        return done_ref[t, b].astype(jnp.int32).astype(F32) * scale
+
     for b in range(members):
         part = slice(b * piece, (b + 1) * piece)
-        w_in_out[part, :] = done_ref[0, b].astype(F32)
-    w_out_out[...] = done_ref[1].astype(F32).reshape(members * piece, width).T
+        w_in_out[part, :] = value(0, b)
+    w_out_out[...] = jnp.concatenate([value(1, b) for b in range(members)], axis=0).T
     b_in_out[...] = b_ref[0:1, :]
     b_out_out[...] = b_ref[1:2, :]
     quarter = dec_out.shape[0] // decs_ref.shape[0]
@@ -578,7 +615,8 @@
         "diff_hbm": diffusion[None, :],
     }
     outputs = {
-        "done": ((2, members, piece, width), BF16),
+        "done": ((2, members, piece, width), jnp.int16),
+        "scale": ((2, members, 1, rows), F32),
         "b_done": ((8, width), F32),
         "decs": ((chunks, quarter + 8, seen_width), F32),
         "cot": ((rows, width), F32),
@@ -609,7 +647,7 @@
         "root": ((rows, rows), F32),
         "len_wide": ((rows, rows), jnp.int32),
         "obs_wide": ((seen_count, rows, rows), jnp.int32),
-        "obs_half": ((seen_count, rows, rows), BF16),
+        "obs_half": ((seen_count, rows, rows), jnp.int16),
         "picked": ((seen_count, rows, width), BF16),
         "misfit": ((seen_count, rows, seen_width), F32),
         "misfit_wide": ((seen_count * rows, width), BF16),
@@ -652,6 +690,7 @@
         "cross_sem": 2,
         "scatter_sem": 2 * (members - 1),
         "spread_sem": 2 * (members - 1),
+        "scale_sem": 2 * (members - 1),
     }
 
     def body(*refs):
@@ -680,17 +719,17 @@
     sem_shapes = [pltpu.SemaphoreType.DMA((len(inputs),))]
     for count in waits.values():
         sem_shapes += [pltpu.SemaphoreType.DMA((count,))] * 2
-    done, b_done, decs, cot, elbo = pl.pallas_call(
+    done, scale, b_done, decs, cot, elbo = pl.pallas_call(
         body,
         out_shape=[jax.ShapeDtypeStruct(*s) for s in outputs.values()],
         in_specs=[hbm] * len(inputs),
         out_specs=[vmem] * len(outputs),
         scratch_shapes=[pltpu.VMEM(*s) for s in scratch.values()] + sem_shapes,
         compiler_params=pltpu.CompilerParams(
-            collective_id=0, has_side_effects=True, vmem_limit_bytes=58 * 1024 * 1024
+            collective_id=0, has_side_effects=True, vmem_limit_bytes=LIMIT
         ),
         name="train",
-    )(*inputs.values())
+    )(*[pltpu.with_memory_space_constraint(v, pltpu.HBM) for v in inputs.values()])
     results = pl.pallas_call(
         finish_kernel,
         out_shape=[
@@ -703,11 +742,11 @@
             jax.ShapeDtypeStruct((rows, width), F32),
             jax.ShapeDtypeStruct((1, rows), F32),
         ],
-        in_specs=[vmem] * 5,
+        in_specs=[vmem] * 6,
         out_specs=[vmem] * 8,
         compiler_params=pltpu.CompilerParams(vmem_limit_bytes=4 * 1024 * 1024),
         name="finish",
-    )(done, b_done, decs, cot, elbo)
+    )(done, scale, b_done, decs, cot, elbo)
     own_w_in, own_w_out, own_b_in, b_out_grad, dec_grad, scores, grad_init, elbo = results
     return (
         elbo[0],

time: 73 us -> 66.8 us (0.915)
  local copies, waits for them, and re-layouts: 4.11 us -> 0 us
  Pallas kernels: 68 us -> 66 us
    unnamed x10 -> x0, local copies, waits for them, and re-layouts: 4.11 us -> none
    pallas_call x1, Pallas kernels: 67 us -> 65 us  [on_device(): pl.pallas_call(body, out_shape=[jax.ShapeDtypeStruct(*s) for s in outputs...]
where the time goes in v3:
time: 66.8 us; the launch traced here: 66.6 us
  Pallas kernels  66 us (99%)
    pallas_call x1, Pallas kernels, on_device(): pl.pallas_call(body, out_shape=[jax.ShapeDtypeStruct(*s) for s in outputs...  65 us

profile of v3, /device:TPU:0, one launch (start us, length us, event | category | flops | bytes accessed | tf_op | source)
XLA Modules:
  0.0 66.6 jit_solution(4456522381212074286)
XLA Ops:
  0.6 65.0 %train.1 = (s16[2,8,32,256]{3,2,1,0:T(8,128)(2,1)S(1)}, f32[2,8,1,128]{3,2,1,0:T(1,128)S(1)}, f32[8,256]{1,0:T(8,128)S(1)}, f32[4,72,128]{2,1,0:T(8,128)S(1)}, f...) custom-call(f32[128,256]{1,0:T(8,128)} %refs_0_.1, bf16[32,128,256]{2,1,0:T(8,128)(2,1)} %refs_1_.1, f32[1,128]{1,0:T(1,128)} %bitcast.14, ...), custom_call_target="tpu_custom_call" | custom-call | tf_op jit(solution)/shard_map/train/pallas_call | solution.py:722
  65.6 1.0 %finish.1 = (f32[256,256]{1,0:T(8,128)}, f32[256,256]{1,0:T(8,128)}, f32[1,256]{1,0:T(1,128)}, f32[1,256]{1,0:T(1,128)}, f32[256,128]{1,0:T(8,128)}, /*index=5*/...) custom-call(s16[2,8,32,256]{3,2,1,0:T(8,128)(2,1)S(1)} %get-tuple-element.22.done_ref, ...), custom_call_target="tpu_custom_call" | custom-call | tf_op jit(solution)/shard_map/finish/pallas_call | solution.py:733

commit v4 on v3

--- a/solution.py
+++ b/solution.py
@@ -58,9 +58,10 @@
     to_sibling, to_across, to_diagonal = (batch, sibling), (batch, across), (batch, diagonal)
     group = (to_sibling, to_across, to_diagonal)
     group_at = (sibling, across, diagonal)
-    others_at = [lax.rem(batch + d, members) for d in range(1, members)]
+    order = sorted(range(1, members), key=lambda d: abs(d - members // 2))
+    others_at = [lax.rem(batch + d, members) for d in order]
     others = [(at, mine) for at in others_at]
-    origins = [lax.rem(batch + members - d, members) for d in range(1, members)]
+    origins = [lax.rem(batch + members - d, members) for d in order]
 
     loads = {}
     for i, (name, source, target) in enumerate(

time: 66.8 us -> 65.7 us (0.984)
  Pallas kernels: 66 us -> 64.9 us
    pallas_call x1, Pallas kernels: 65 us -> 63.9 us  [on_device(): pl.pallas_call(body, out_shape=[jax.ShapeDtypeStruct(*s) for s in outputs...]
where the time goes in v4:
time: 65.7 us; the launch traced here: 65.5 us
  Pallas kernels  64.9 us (99%)
    pallas_call x1, Pallas kernels, on_device(): pl.pallas_call(body, out_shape=[jax.ShapeDtypeStruct(*s) for s in outputs...  63.9 us

profile of v4, /device:TPU:0, one launch (start us, length us, event | category | flops | bytes accessed | tf_op | source)
XLA Modules:
  0.0 65.5 jit_solution(13885581004295044697)
XLA Ops:
  0.6 63.9 %train.1 = (s16[2,8,32,256]{3,2,1,0:T(8,128)(2,1)S(1)}, f32[2,8,1,128]{3,2,1,0:T(1,128)S(1)}, f32[8,256]{1,0:T(8,128)S(1)}, f32[4,72,128]{2,1,0:T(8,128)S(1)}, f...) custom-call(f32[128,256]{1,0:T(8,128)} %refs_0_.1, bf16[32,128,256]{2,1,0:T(8,128)(2,1)} %refs_1_.1, f32[1,128]{1,0:T(1,128)} %bitcast.14, ...), custom_call_target="tpu_custom_call" | custom-call | tf_op jit(solution)/shard_map/train/pallas_call | solution.py:723
  64.6 1.0 %finish.1 = (f32[256,256]{1,0:T(8,128)}, f32[256,256]{1,0:T(8,128)}, f32[1,256]{1,0:T(1,128)}, f32[1,256]{1,0:T(1,128)}, f32[256,128]{1,0:T(8,128)}, /*index=5*/...) custom-call(s16[2,8,32,256]{3,2,1,0:T(8,128)(2,1)S(1)} %get-tuple-element.22.done_ref, ...), custom_call_target="tpu_custom_call" | custom-call | tf_op jit(solution)/shard_map/finish/pallas_call | solution.py:734
